TPU v7x, 32 devices: a whole 2x2x4 slice. The times are simulated.
32 devices in a mesh: tm: 8 (over z, y), space: 4 (over x, core).
Axes of the slice: x: 2, y: 2, z: 4, core: 2. Of those that a mesh axis runs over, the one named last changes fastest.
Arguments:
- observed: float32 [64, 512, 128], P('tm', 'space'), may hold values from -6 to 6
- gain: float32 [4, 128, 128], P('space'), may hold values from -0.15625 to 0.15625
- trans: float32 [4, 384, 128], P('space'), may hold values from -1 to 1
- dynamics: float32 [4, 384, 128], P('space'), may hold values from -1 to 1
- smooth_gain: float32 [4, 384, 128], P('space'), may hold values from -1 to 1
Outputs:
- filtered: float32 [64, 512, 128], P('tm', 'space')
- smoothed: float32 [64, 512, 128], P('tm', 'space')
All inputs are finite; a program needn't handle non-finite values.
Results may differ from a plain program's by a relative error of at most 0.00017.
Values sent between devices are 32-bit elements; how exact they have to be, the bound alone decides.
A program may use at most 128 MiB of HBM per device.

v0:
```python
from functools import partial

import jax
import jax.numpy as jnp
from jax import lax
from jax.experimental import pallas as pl
from jax.experimental.pallas import tpu as pltpu
from jax.sharding import PartitionSpec as P

highest_mode = lax.Precision.HIGHEST


def shifted(shard, axis, by):
    devices = lax.axis_size(axis)
    pairs = [(i, i + by) for i in range(devices) if 0 <= i + by < devices]
    return lax.ppermute(shard, axis, pairs)


def apply_full(banded, current):
    count_tiles = banded.shape[0]
    tile_width = banded.shape[2]
    blocks = current.reshape(current.shape[0], count_tiles, tile_width, current.shape[2])
    empty_tile = jnp.zeros_like(blocks[:, :1])
    padded = jnp.concatenate([empty_tile, blocks, empty_tile], 1)
    stacked = jnp.concatenate([padded[:, :-2], padded[:, 1:-1], padded[:, 2:]], 2)
    result = jnp.einsum("crs,ncre->ncse", banded, stacked, precision=highest_mode)
    return result.reshape(current.shape)


def sweep(apply_step, inputs, entry, backward):
    length = inputs.shape[0]
    order = list(range(length - 1, -1, -1)) if backward else list(range(length))
    current = entry
    outputs = [entry] * length
    for moment in order:
        current = apply_step(current[None])[0] + inputs[moment]
        outputs[moment] = current
    return jnp.stack(outputs)


def carry_prefix(carry, tables, which, direction):
    total = carry
    for level in range(len(tables) + 1):
        reach = direction * (1 if level == 0 else 2 ** (level - 1))
        moved = shifted(total, "tm", reach)
        if level == 0:
            total = moved
        else:
            table = tables[level - 1][which]

            def term(start, count, table=table, moved=moved):
                return lax.dot_general(
                    table, moved, (((0,), (0,)), ((), ())), precision=highest_mode
                )

            total = total + lax.psum_scatter(
                term(jnp.int32(0), moved.shape[0] * lax.axis_size("space")),
                "space",
                scatter_dimension=0,
                tiled=True,
            )
    return total


def body(observed, gain, trans, dynamics, smooth_gain):
    steps, tile_width, members = observed.shape
    count_tiles = lax.axis_size("space")
    ranks = lax.axis_size("tm")
    place = lax.axis_index("tm")
    column = lax.axis_index("space")
    state_width = tile_width * count_tiles
    block_cols = state_width // ranks
    sections = (ranks - 1).bit_length()
    log_steps = steps.bit_length() - 1
    forcing = jnp.einsum("os,toe->tse", gain[0], observed, precision=highest_mode)
    full_trans, full_smooth, full_dynamics = (
        lax.all_gather(trans, "space", axis=0, tiled=True),
        lax.all_gather(smooth_gain, "space", axis=0, tiled=True),
        lax.all_gather(dynamics, "space", axis=0, tiled=True),
    )

    def first_block(full):
        target = place * block_cols // tile_width
        offset = place * block_cols % tile_width
        index = jnp.clip(target, 0, full.shape[0] - 1)
        slab = lax.dynamic_index_in_dim(full, index, 0, keepdims=False)
        row_start = jnp.clip(column - target + 1, 0, 2) * tile_width
        piece = lax.dynamic_slice(slab, (row_start, offset), (tile_width, block_cols))
        inside = (jnp.abs(column - target) <= 1).astype(jnp.float32)
        return piece * inside

    blocks = (first_block(full_trans), first_block(full_smooth))
    needed = []
    for level in range(log_steps + sections - 1):
        col_trans = lax.all_gather(blocks[0], "space", axis=0, tiled=True)
        col_smooth = lax.all_gather(blocks[1], "space", axis=0, tiled=True)
        blocks = (
            jnp.dot(
                lax.all_gather(blocks[0], "tm", axis=1, tiled=True),
                col_trans,
                precision=highest_mode,
            ),
            jnp.dot(
                lax.all_gather(blocks[1], "tm", axis=1, tiled=True),
                col_smooth,
                precision=highest_mode,
            ),
        )
        if level + 1 >= log_steps:
            needed.append(blocks)
    tables = []
    for pair in needed:
        tables.append(
            (
                lax.all_gather(pair[0], "tm", axis=1, tiled=True),
                lax.all_gather(pair[1], "tm", axis=1, tiled=True),
            )
        )
    final_moment = jnp.arange(steps)[:, None, None] == steps - 1
    at_end = jnp.logical_and(final_moment, place == ranks - 1)
    whole_forcing = lax.all_gather(forcing, "space", axis=1, tiled=True)
    zero_full = jnp.zeros((state_width, members), jnp.float32)
    step_trans = partial(apply_full, full_trans)
    step_smooth = partial(apply_full, full_smooth)
    trial = sweep(step_trans, whole_forcing, zero_full, False)
    own_tail = lax.dynamic_slice_in_dim(trial[steps - 1], column * tile_width, tile_width, 0)
    entry = carry_prefix(own_tail, tables, 0, 1)
    entry_full = lax.all_gather(entry, "space", axis=0, tiled=True)
    filtered_full = sweep(step_trans, whole_forcing, entry_full, False)
    mixed_full = apply_full(full_smooth, apply_full(full_dynamics, filtered_full))
    innovation_full = jnp.where(at_end, filtered_full, filtered_full - mixed_full)
    trial_back = sweep(step_smooth, innovation_full, zero_full, True)
    own_head = lax.dynamic_slice_in_dim(trial_back[0], column * tile_width, tile_width, 0)
    exit_state = carry_prefix(own_head, tables, 1, -1)
    exit_full = lax.all_gather(exit_state, "space", axis=0, tiled=True)
    smoothed_full = sweep(step_smooth, innovation_full, exit_full, True)
    filtered = lax.dynamic_slice_in_dim(filtered_full, column * tile_width, tile_width, 1)
    smoothed = lax.dynamic_slice_in_dim(smoothed_full, column * tile_width, tile_width, 1)
    return (filtered, smoothed)

MESH = pl.DeviceIdType.MESH
SUBLANES = 8
SPLIT = (1, 2)


def pieces(x):
    high = x.astype(jnp.bfloat16)
    return high, (x - high.astype(jnp.float32)).astype(jnp.bfloat16)


def dot(a, b):
    return jnp.dot(a, b, preferred_element_type=jnp.float32)


def times(x, table):
    rows = x.shape[0]
    high = x.astype(jnp.bfloat16).astype(jnp.float32)
    both = jnp.concatenate([high, x - high], 0).astype(jnp.bfloat16)
    two = dot(both, table[0]) + dot(both, table[1])
    return two[:rows] + two[rows:]


def square(table, result):
    width = table.shape[1]
    part = min(width, 256)

    def one(index, _):
        rows = pl.ds(pl.multiple_of(index * part, part), part)
        high, low = table[0, rows, :], table[1, rows, :]
        two = dot(jnp.concatenate([high, low], 0), table[0])
        total = two[:part] + (two[part:] + dot(high, table[1]))
        for place, piece in enumerate(pieces(total)):
            result[place, rows, :] = piece
        return 0

    lax.fori_loop(0, width // part, one, 0)


def swap_halves(x):
    return pltpu.roll(x, SUBLANES // 2, x.ndim - 2)


def upper_half(shape):
    return lax.broadcasted_iota(jnp.int32, shape, len(shape) - 2) < SUBLANES // 2


def interleave(first, second):
    upper = upper_half(first.shape)
    return (
        jnp.where(upper, first, swap_halves(second)),
        jnp.where(upper, swap_halves(first), second),
    )


def kernel(
    ranks, columns, observed, gain, trans, dynamics, smooth_gain, filtered, smoothed,
    outbox, forcing, states, drive, results, inbox_f, inbox_s, entries, summed, raw,
    trans_1, trans_p, trans_4, trans_8, smooth_1, smooth_4, smooth_8, dyn_1,
    table_send, table_recv, table_own, force_send, force_recv, filt_send, filt_recv, smoo_send, smoo_recv, own_sem,
):
    steps, tile_width, members = observed.shape
    devices = ranks * columns
    short = steps // 2
    state_width = columns * tile_width
    rank = lax.axis_index("tm")
    column = lax.axis_index("space")
    me = rank * columns + column
    beside = column + 1 - 2 * (column % 2)
    across = (column + 2) % columns

    barrier = pltpu.get_barrier_semaphore()

    def greet(offset, _):
        other = (me + offset) % devices
        pl.semaphore_signal(
            barrier, inc=1, device_id=(other // columns, other % columns), device_id_type=MESH
        )
        return 0

    lax.fori_loop(1, devices, greet, 0)

    sources = (trans, smooth_gain, dynamics)
    for which, source in enumerate(sources):
        pltpu.make_async_copy(source.at[0], raw.at[which, column], table_own.at[which]).start()

    groups = members // SUBLANES

    gain_high, gain_low = pieces(gain[0])

    def force(step, _):
        halves = []
        for half in range(2):
            image = observed[half * short + step].T
            high, low = pieces(image)
            value = dot(high, gain_high) + (dot(low, gain_high) + dot(high, gain_low))
            halves.append(value.reshape(groups, SUBLANES, tile_width))
        even, odd = interleave(*halves)
        outbox[:, 0, pl.ds(step, 1)] = even[:, None]
        outbox[:, 1, pl.ds(step, 1)] = odd[:, None]
        return 0

    lax.fori_loop(0, short, force, 0)
    pl.semaphore_wait(barrier, devices - 1)

    shared = rank % 2
    partner = rank + 1 - 2 * shared

    def half_rows(index):
        count = 3 * tile_width // 2
        return pl.ds(pl.multiple_of(index * count, count), count)

    def table_copy(which, what):
        split = which in SPLIT
        if what == 0:
            place, to = column, (rank, across)
            rows = half_rows(shared) if split else slice(None)
        elif what == 1:
            place, to, rows = column, (rank, beside), slice(None)
        elif what == 2:
            place, to = across, (rank, beside)
            rows = half_rows(shared) if split else slice(None)
        elif what == 3:
            place, to, rows = across, (partner, column), half_rows(shared)
        else:
            place, to, rows = across, (rank, beside), half_rows(1 - shared)
        source = sources[which].at[0, rows] if what < 2 else raw.at[which, place, rows]
        return pltpu.make_async_remote_copy(
            src_ref=source,
            dst_ref=raw.at[which, place, rows],
            send_sem=table_send.at[which, what],
            recv_sem=table_recv.at[which, what],
            device_id=to,
            device_id_type=MESH,
        )

    def send_table(which):
        table_copy(which, 0).start()
        table_copy(which, 1).start()

    def relay_table(which):
        table_copy(which, 0).wait_recv()
        table_copy(which, 2).start()
        if which in SPLIT:
            table_copy(which, 3).start()

    def relay_again(which):
        if which in SPLIT:
            table_copy(which, 3).wait_recv()
            table_copy(which, 4).start()

    def finish_table(which):
        pltpu.make_async_copy(sources[which].at[0], raw.at[which, column], table_own.at[which]).wait()
        table_copy(which, 1).wait_recv()
        table_copy(which, 2).wait_recv()
        if which in SPLIT:
            table_copy(which, 4).wait_recv()

    def build(which, table):
        for tile in range(columns):
            lanes = slice(tile * tile_width, (tile + 1) * tile_width)
            for row in range(columns):
                rows = slice(row * tile_width, (row + 1) * tile_width)
                shift = row - tile + 1
                if 0 <= shift <= 2:
                    block = raw[which, tile, shift * tile_width : (shift + 1) * tile_width, :]
                    for place, piece in enumerate(pieces(block)):
                        table[place, rows, lanes] = piece
                else:
                    for place in range(2):
                        table[place, rows, lanes] = jnp.zeros((tile_width, tile_width), jnp.bfloat16)

    def lane_part(index):
        return pl.ds(pl.multiple_of(index * tile_width, tile_width), tile_width)

    def force_copy(offset):
        other = (me + offset) % devices
        return pltpu.make_async_remote_copy(
            src_ref=outbox.at[other // 2, other % 2],
            dst_ref=forcing.at[:, rank, :, lane_part(column)],
            send_sem=force_send.at[offset],
            recv_sem=force_recv.at[offset],
            device_id=(other // columns, other % columns),
            device_id_type=MESH,
        )

    def result_copy(offset, source, inbox, send, recv):
        other = (me + offset) % devices
        return pltpu.make_async_remote_copy(
            src_ref=source.at[:, other // columns, :, lane_part(other % columns)],
            dst_ref=inbox.at[me // 2, me % 2],
            send_sem=send.at[offset],
            recv_sem=recv.at[offset],
            device_id=(other // columns, other % columns),
            device_id_type=MESH,
        )

    def over_others(act):
        def one(offset, _):
            act(offset)
            return 0

        lax.fori_loop(1, devices, one, 0)

    send_table(0)
    over_others(lambda offset: force_copy(offset).start())
    own_force = pltpu.make_async_copy(
        outbox.at[me // 2, me % 2], forcing.at[:, rank, :, lane_part(column)], own_sem.at[0]
    )
    own_force.start()
    send_table(1)
    send_table(2)

    relay_table(0)
    finish_table(0)
    build(0, trans_1)
    square(trans_1, trans_p)
    square(trans_p, trans_4)
    square(trans_4, trans_8)
    over_others(lambda offset: force_copy(offset).wait_recv())
    own_force.wait()

    relay_table(1)
    rows = ranks * SUBLANES
    whole = (ranks, SUBLANES, state_width)

    def flat(x):
        return x.reshape(rows, state_width)

    def trial(inputs, order, table):
        def one(index, current):
            return times(current, table) + flat(inputs[order(index)])

        return lax.fori_loop(1, short, one, flat(inputs[order(0)]))

    def chain(order, table):
        entries[order(0)] = jnp.zeros((SUBLANES, state_width), jnp.float32)
        entries[order(1)] = summed[order(0)]

        def one(index, current):
            current = times(current, table) + summed[order(index)]
            entries[order(index + 1)] = current
            return current

        lax.fori_loop(1, ranks - 1, one, summed[order(0)])

    def final(inputs, order, table, entry, outputs):
        def one(index, current):
            current = times(current, table) + flat(inputs[order(index)])
            outputs[order(index)] = current.reshape(whole)
            return current

        lax.fori_loop(0, short, one, entry)

    forward = lambda index: index
    upper = upper_half(whole)
    ends = trial(forcing, forward, trans_1)
    halves = ends.reshape(whole)
    summed[...] = times(ends, trans_4).reshape(whole) + swap_halves(halves)
    relay_table(2)
    relay_again(1)
    chain(forward, trans_8)
    first = entries[...]
    second = times(flat(first), trans_4).reshape(whole) + halves
    relay_again(2)
    final(forcing, forward, trans_1, flat(jnp.where(upper, first, swap_halves(second))), states)

    over_others(lambda offset: result_copy(offset, states, inbox_f, filt_send, filt_recv).start())
    own_filtered = pltpu.make_async_copy(
        states.at[:, rank, :, lane_part(column)], inbox_f.at[me // 2, me % 2], own_sem.at[1]
    )
    own_filtered.start()

    finish_table(1)
    build(1, smooth_1)
    square(smooth_1, trans_p)
    square(trans_p, smooth_4)
    square(smooth_4, smooth_8)
    finish_table(2)
    build(2, dyn_1)

    def innovate(step, _):
        value = flat(states[step])
        mixed = times(times(value, dyn_1), smooth_1)
        place = lax.broadcasted_iota(jnp.int32, mixed.shape, 0)
        at_end = jnp.logical_and(place >= rows - SUBLANES // 2, step == short - 1)
        drive[step] = jnp.where(at_end, value, value - mixed).reshape(whole)
        return 0

    lax.fori_loop(0, short, innovate, 0)

    backward = lambda index: short - 1 - index
    heads = trial(drive, backward, smooth_1)
    halves = heads.reshape(whole)
    summed[...] = swap_halves(times(heads, smooth_4).reshape(whole)) + halves
    chain(lambda index: ranks - 1 - index, smooth_8)
    last = entries[...]
    before = times(flat(last), smooth_4).reshape(whole) + swap_halves(halves)
    final(drive, backward, smooth_1, flat(jnp.where(upper, before, swap_halves(last))), results)

    over_others(lambda offset: result_copy(offset, results, inbox_s, smoo_send, smoo_recv).start())
    own_smoothed = pltpu.make_async_copy(
        results.at[:, rank, :, lane_part(column)], inbox_s.at[me // 2, me % 2], own_sem.at[2]
    )
    own_smoothed.start()

    def deliver(inbox, output):
        def one(step, _):
            parts = interleave(inbox[:, 0, step], inbox[:, 1, step])
            for half, part in enumerate(parts):
                output[half * short + step] = part.reshape(members, tile_width).T
            return 0

        lax.fori_loop(0, short, one, 0)

    over_others(lambda offset: result_copy(offset, states, inbox_f, filt_send, filt_recv).wait_recv())
    own_filtered.wait()
    deliver(inbox_f, filtered)
    over_others(lambda offset: result_copy(offset, results, inbox_s, smoo_send, smoo_recv).wait_recv())
    own_smoothed.wait()
    deliver(inbox_s, smoothed)

    for which in range(3):
        for what in range(5 if which in SPLIT else 3):
            table_copy(which, what).wait_send()
    over_others(lambda offset: force_copy(offset).wait_send())
    over_others(lambda offset: result_copy(offset, states, inbox_f, filt_send, filt_recv).wait_send())
    over_others(lambda offset: result_copy(offset, results, inbox_s, smoo_send, smoo_recv).wait_send())


def member_body(ranks, columns, observed, gain, trans, dynamics, smooth_gain):
    steps, tile_width, members = observed.shape
    devices = ranks * columns
    short = steps // 2
    width = columns * tile_width
    pairs = devices // 2
    boxes = pltpu.VMEM((pairs, 2, short, SUBLANES, tile_width), jnp.float32)
    series = pltpu.VMEM((short, ranks, SUBLANES, width), jnp.float32)
    block = pltpu.VMEM((ranks, SUBLANES, width), jnp.float32)
    table = pltpu.VMEM((2, width, width), jnp.bfloat16)
    each = pltpu.SemaphoreType.DMA((devices,))
    vmem = pl.BlockSpec(memory_space=pltpu.VMEM)
    return pl.pallas_call(
        partial(kernel, ranks, columns),
        out_shape=[jax.ShapeDtypeStruct(observed.shape, jnp.float32)] * 2,
        in_specs=[vmem] * 5,
        out_specs=[vmem] * 2,
        scratch_shapes=[
            boxes, series, series, series, series, boxes, boxes, block, block,
            pltpu.VMEM((3, columns, 3 * tile_width, tile_width), jnp.float32),
            table, table, table, table, table, table, table, table,
            pltpu.SemaphoreType.DMA((3, 5)),
            pltpu.SemaphoreType.DMA((3, 5)),
            pltpu.SemaphoreType.DMA((3,)),
            each, each, each, each, each, each,
            pltpu.SemaphoreType.DMA((3,)),
        ],
        compiler_params=pltpu.CompilerParams(
            collective_id=0, has_side_effects=True, vmem_limit_bytes=56 * 2**20
        ),
    )(observed, gain, trans, dynamics, smooth_gain)


def by_members(mesh, observed, gain, trans, dynamics, smooth_gain):
    ranks, columns = mesh.shape["tm"], mesh.shape["space"]
    devices = ranks * columns
    steps, tile_width, members = observed.shape
    fits = (
        members * 2 == devices * SUBLANES
        and steps % 2 == 0
        and columns == 4
        and ranks >= 3
        and tile_width == 128
        and members == 128
    )
    if fits:
        return tuple(member_body(ranks, columns, observed, gain, trans, dynamics, smooth_gain))
    return body(observed, gain, trans, dynamics, smooth_gain)


def solution(mesh):
    return jax.shard_map(
        partial(by_members, mesh),
        mesh=mesh,
        in_specs=(
            P("tm", "space", None),
            P("space", None, None),
            P("space", None, None),
            P("space", None, None),
            P("space", None, None),
        ),
        out_specs=(P("tm", "space", None), P("tm", "space", None)),
        check_vma=False,
    )
```

profile of v0, /device:TPU:15, one launch (start us, length us, event | category | flops | bytes accessed | tf_op | source)
XLA Modules:
  0.0 59.5 jit_solution(8762282189873110575)
XLA Ops:
  0.6 56.1 %shard_map.68 = (f32[8,128,128]{2,1,0:T(8,128)}, f32[8,128,128]{2,1,0:T(8,128)}) custom-call(f32[8,128,128]{2,1,0:T(8,128)} %observed.1, f32[1,128,128]{2,1,0:T(8,128)} %gain.1, f32[1,384,128]{2,1,0:T(8,128)} %trans.1, f32[1,384,128]{2,1,0:T(8,128)} %dynamics.1, f32[1,384,128]{2,1,0:T(8,128)} %smooth_gain.1), custom_call_target="tpu_custom_call" | custom-call | tf_op jit(solution)/shard_map/pallas_call | solution.py:482
  56.7 0.0 copy-start
  56.7 1.9 %copy.9 = f32[8,128,128]{2,1,0:T(8,128)} copy(f32[8,128,128]{2,1,0:T(8,128)} %get-tuple-element.4) | data formatting | bytes 1048576
  58.7 0.0 copy-done
  58.7 0.8 %copy.10 = f32[8,128,128]{2,1,0:T(8,128)} copy(f32[8,128,128]{2,1,0:T(8,128)S(1)} %copy-done) | data formatting | bytes 1048576
Async XLA Ops:
  56.7 1.9 %copy-start = (f32[8,128,128]{2,1,0:T(8,128)S(1)}, f32[8,128,128]{2,1,0:T(8,128)}, u32[]{:S(2)}) copy-start(f32[8,128,128]{2,1,0:T(8,128)} %get-tuple-element.5) | copy-start | bytes 1572868
where the time goes:
time: 59.6 us; the launch traced here: 59.5 us
  Pallas kernels  56.1 us (94%)
  local copies, waits for them, and re-layouts  2.73 us (5%)
  between operations  0.65 us (1%)
    pallas_call x1, Pallas kernels, member_body(): pl.pallas_call(partial(kernel, ranks, columns), out_shape=[jax.ShapeDtype...  56.1 us
    unnamed x4, local copies, waits for them, and re-layouts  2.73 us

commit v1 on v0

v1 whole, which is shorter than its diff:
```python
from functools import partial

import jax
import jax.numpy as jnp
from jax import lax
from jax.experimental import pallas as pl
from jax.experimental.pallas import tpu as pltpu
from jax.sharding import PartitionSpec as P

highest_mode = lax.Precision.HIGHEST


def shifted(shard, axis, by):
    devices = lax.axis_size(axis)
    pairs = [(i, i + by) for i in range(devices) if 0 <= i + by < devices]
    return lax.ppermute(shard, axis, pairs)


def apply_full(banded, current):
    count_tiles = banded.shape[0]
    tile_width = banded.shape[2]
    blocks = current.reshape(current.shape[0], count_tiles, tile_width, current.shape[2])
    empty_tile = jnp.zeros_like(blocks[:, :1])
    padded = jnp.concatenate([empty_tile, blocks, empty_tile], 1)
    stacked = jnp.concatenate([padded[:, :-2], padded[:, 1:-1], padded[:, 2:]], 2)
    result = jnp.einsum("crs,ncre->ncse", banded, stacked, precision=highest_mode)
    return result.reshape(current.shape)


def sweep(apply_step, inputs, entry, backward):
    length = inputs.shape[0]
    order = list(range(length - 1, -1, -1)) if backward else list(range(length))
    current = entry
    outputs = [entry] * length
    for moment in order:
        current = apply_step(current[None])[0] + inputs[moment]
        outputs[moment] = current
    return jnp.stack(outputs)


def carry_prefix(carry, tables, which, direction):
    total = carry
    for level in range(len(tables) + 1):
        reach = direction * (1 if level == 0 else 2 ** (level - 1))
        moved = shifted(total, "tm", reach)
        if level == 0:
            total = moved
        else:
            table = tables[level - 1][which]

            def term(start, count, table=table, moved=moved):
                return lax.dot_general(
                    table, moved, (((0,), (0,)), ((), ())), precision=highest_mode
                )

            total = total + lax.psum_scatter(
                term(jnp.int32(0), moved.shape[0] * lax.axis_size("space")),
                "space",
                scatter_dimension=0,
                tiled=True,
            )
    return total


def body(observed, gain, trans, dynamics, smooth_gain):
    steps, tile_width, members = observed.shape
    count_tiles = lax.axis_size("space")
    ranks = lax.axis_size("tm")
    place = lax.axis_index("tm")
    column = lax.axis_index("space")
    state_width = tile_width * count_tiles
    block_cols = state_width // ranks
    sections = (ranks - 1).bit_length()
    log_steps = steps.bit_length() - 1
    forcing = jnp.einsum("os,toe->tse", gain[0], observed, precision=highest_mode)
    full_trans, full_smooth, full_dynamics = (
        lax.all_gather(trans, "space", axis=0, tiled=True),
        lax.all_gather(smooth_gain, "space", axis=0, tiled=True),
        lax.all_gather(dynamics, "space", axis=0, tiled=True),
    )

    def first_block(full):
        target = place * block_cols // tile_width
        offset = place * block_cols % tile_width
        index = jnp.clip(target, 0, full.shape[0] - 1)
        slab = lax.dynamic_index_in_dim(full, index, 0, keepdims=False)
        row_start = jnp.clip(column - target + 1, 0, 2) * tile_width
        piece = lax.dynamic_slice(slab, (row_start, offset), (tile_width, block_cols))
        inside = (jnp.abs(column - target) <= 1).astype(jnp.float32)
        return piece * inside

    blocks = (first_block(full_trans), first_block(full_smooth))
    needed = []
    for level in range(log_steps + sections - 1):
        col_trans = lax.all_gather(blocks[0], "space", axis=0, tiled=True)
        col_smooth = lax.all_gather(blocks[1], "space", axis=0, tiled=True)
        blocks = (
            jnp.dot(
                lax.all_gather(blocks[0], "tm", axis=1, tiled=True),
                col_trans,
                precision=highest_mode,
            ),
            jnp.dot(
                lax.all_gather(blocks[1], "tm", axis=1, tiled=True),
                col_smooth,
                precision=highest_mode,
            ),
        )
        if level + 1 >= log_steps:
            needed.append(blocks)
    tables = []
    for pair in needed:
        tables.append(
            (
                lax.all_gather(pair[0], "tm", axis=1, tiled=True),
                lax.all_gather(pair[1], "tm", axis=1, tiled=True),
            )
        )
    final_moment = jnp.arange(steps)[:, None, None] == steps - 1
    at_end = jnp.logical_and(final_moment, place == ranks - 1)
    whole_forcing = lax.all_gather(forcing, "space", axis=1, tiled=True)
    zero_full = jnp.zeros((state_width, members), jnp.float32)
    step_trans = partial(apply_full, full_trans)
    step_smooth = partial(apply_full, full_smooth)
    trial = sweep(step_trans, whole_forcing, zero_full, False)
    own_tail = lax.dynamic_slice_in_dim(trial[steps - 1], column * tile_width, tile_width, 0)
    entry = carry_prefix(own_tail, tables, 0, 1)
    entry_full = lax.all_gather(entry, "space", axis=0, tiled=True)
    filtered_full = sweep(step_trans, whole_forcing, entry_full, False)
    mixed_full = apply_full(full_smooth, apply_full(full_dynamics, filtered_full))
    innovation_full = jnp.where(at_end, filtered_full, filtered_full - mixed_full)
    trial_back = sweep(step_smooth, innovation_full, zero_full, True)
    own_head = lax.dynamic_slice_in_dim(trial_back[0], column * tile_width, tile_width, 0)
    exit_state = carry_prefix(own_head, tables, 1, -1)
    exit_full = lax.all_gather(exit_state, "space", axis=0, tiled=True)
    smoothed_full = sweep(step_smooth, innovation_full, exit_full, True)
    filtered = lax.dynamic_slice_in_dim(filtered_full, column * tile_width, tile_width, 1)
    smoothed = lax.dynamic_slice_in_dim(smoothed_full, column * tile_width, tile_width, 1)
    return (filtered, smoothed)

MESH = pl.DeviceIdType.MESH
SUBLANES = 8
SPLIT = (0, 1, 2)


def pieces(x):
    high = x.astype(jnp.bfloat16)
    return high, (x - high.astype(jnp.float32)).astype(jnp.bfloat16)


def dot(a, b):
    return jnp.dot(a, b, preferred_element_type=jnp.float32)


def times(x, table):
    rows = x.shape[0]
    high = x.astype(jnp.bfloat16).astype(jnp.float32)
    both = jnp.concatenate([high, x - high], 0).astype(jnp.bfloat16)
    two = dot(both, table[0])
    return two[:rows] + (two[rows:] + dot(both[:rows], table[1]))


def product(left, right, result):
    width = left.shape[1]
    part = min(width, 256)
    for start in range(0, width, part):
        rows = slice(start, start + part)
        high, low = left[0, rows, :], left[1, rows, :]
        two = dot(jnp.concatenate([high, low], 0), right[0])
        total = two[:part] + (two[part:] + dot(high, right[1]))
        for place, piece in enumerate(pieces(total)):
            result[place, rows, :] = piece


def kernel(
    ranks, columns, observed, gain, trans, dynamics, smooth_gain, filtered, smoothed,
    outbox, forcing, states, drive, results, inbox_f, inbox_s, ends, sums, firsts, edge, carry, raw,
    trans_1, trans_2, trans_4, trans_8, smooth_1, smooth_2, smooth_4, smooth_8, dyn_1, mix_1,
    table_send, table_recv, table_own, force_send, force_recv, filt_send, filt_recv, smoo_send, smoo_recv,
    carry_send, carry_recv, own_sem,
):
    steps, tile_width, members = observed.shape
    short = steps // 2
    span = ranks // 2
    group = span * columns
    subs = 2 * span
    rows = subs * SUBLANES
    state_width = columns * tile_width
    rank = lax.axis_index("tm")
    column = lax.axis_index("space")
    half = rank // span
    local = rank % span
    me = local * columns + column
    beside = column + 1 - 2 * (column % 2)
    across = (column + 2) % columns
    early = half == 0
    late = half == 1

    barrier = pltpu.get_barrier_semaphore()

    def member(offset):
        other = (me + offset) % group
        return other // columns, other % columns

    def greet(offset, _):
        place, lane = member(offset)
        pl.semaphore_signal(
            barrier, inc=1, device_id=(half * span + place, lane), device_id_type=MESH
        )
        return 0

    lax.fori_loop(1, group, greet, 0)
    opposite = (rank + span) % ranks
    pl.semaphore_signal(barrier, inc=1, device_id=(opposite, column), device_id_type=MESH)

    sources = (trans, smooth_gain, dynamics)
    for which, source in enumerate(sources):
        pltpu.make_async_copy(source.at[0], raw.at[which, column], table_own.at[which]).start()

    gain_high, gain_low = pieces(gain[0])

    def force(step, _):
        for part in range(2):
            image = observed[part * short + step].T
            high, low = pieces(image)
            value = dot(high, gain_high) + (dot(low, gain_high) + dot(high, gain_low))
            outbox[:, pl.ds(step, 1), part] = value.reshape(group, 1, SUBLANES, tile_width)
        return 0

    lax.fori_loop(0, short, force, 0)
    pl.semaphore_wait(barrier, group)

    shared = rank % 2
    partner = rank + 1 - 2 * shared

    def half_rows(index):
        count = 3 * tile_width // 2
        return pl.ds(pl.multiple_of(index * count, count), count)

    def table_copy(which, what):
        split = which in SPLIT
        if what == 0:
            place, to = column, (rank, across)
            part = half_rows(shared) if split else slice(None)
        elif what == 1:
            place, to, part = column, (rank, beside), slice(None)
        elif what == 2:
            place, to = across, (rank, beside)
            part = half_rows(shared) if split else slice(None)
        elif what == 3:
            place, to, part = across, (partner, column), half_rows(shared)
        else:
            place, to, part = across, (rank, beside), half_rows(1 - shared)
        source = sources[which].at[0, part] if what < 2 else raw.at[which, place, part]
        return pltpu.make_async_remote_copy(
            src_ref=source,
            dst_ref=raw.at[which, place, part],
            send_sem=table_send.at[which, what],
            recv_sem=table_recv.at[which, what],
            device_id=to,
            device_id_type=MESH,
        )

    def send_table(which):
        table_copy(which, 0).start()
        table_copy(which, 1).start()

    def relay_table(which):
        table_copy(which, 0).wait_recv()
        if which in SPLIT:
            table_copy(which, 3).start()
        table_copy(which, 2).start()

    def relay_again(which):
        if which in SPLIT:
            table_copy(which, 3).wait_recv()
            table_copy(which, 4).start()

    def finish_table(which):
        pltpu.make_async_copy(sources[which].at[0], raw.at[which, column], table_own.at[which]).wait()
        table_copy(which, 1).wait_recv()
        table_copy(which, 2).wait_recv()
        if which in SPLIT:
            table_copy(which, 4).wait_recv()

    def build(which, table):
        for tile in range(columns):
            lanes = slice(tile * tile_width, (tile + 1) * tile_width)
            for row in range(columns):
                part = slice(row * tile_width, (row + 1) * tile_width)
                shift = row - tile + 1
                if 0 <= shift <= 2:
                    block = raw[which, tile, shift * tile_width : (shift + 1) * tile_width, :]
                    for place, piece in enumerate(pieces(block)):
                        table[place, part, lanes] = piece
                else:
                    for place in range(2):
                        table[place, part, lanes] = jnp.zeros((tile_width, tile_width), jnp.bfloat16)

    def lane_part(index):
        return pl.ds(pl.multiple_of(index * tile_width, tile_width), tile_width)

    def force_copy(offset):
        place, lane = member(offset)
        return pltpu.make_async_remote_copy(
            src_ref=outbox.at[(me + offset) % group],
            dst_ref=forcing.at[:, pl.ds(2 * local, 2), :, lane_part(column)],
            send_sem=force_send.at[offset],
            recv_sem=force_recv.at[offset],
            device_id=(half * span + place, lane),
            device_id_type=MESH,
        )

    def result_copy(offset, source, inbox, send, recv):
        place, lane = member(offset)
        return pltpu.make_async_remote_copy(
            src_ref=source.at[:, pl.ds(2 * place, 2), :, lane_part(lane)],
            dst_ref=inbox.at[me],
            send_sem=send.at[offset],
            recv_sem=recv.at[offset],
            device_id=(half * span + place, lane),
            device_id_type=MESH,
        )

    def own_result(source, inbox, index):
        return pltpu.make_async_copy(
            source.at[:, pl.ds(2 * local, 2), :, lane_part(column)], inbox.at[me], own_sem.at[index]
        )

    def carry_copy(index):
        return pltpu.make_async_remote_copy(
            src_ref=edge.at[index],
            dst_ref=carry.at[index],
            send_sem=carry_send.at[index],
            recv_sem=carry_recv.at[index],
            device_id=(opposite, column),
            device_id_type=MESH,
        )

    def over_others(act):
        def one(offset, _):
            act(offset)
            return 0

        lax.fori_loop(1, group, one, 0)

    filtered_copy = lambda offset: result_copy(offset, states, inbox_f, filt_send, filt_recv)
    smoothed_copy = lambda offset: result_copy(offset, results, inbox_s, smoo_send, smoo_recv)

    send_table(0)
    over_others(lambda offset: force_copy(offset).start())
    own_force = pltpu.make_async_copy(
        outbox.at[me], forcing.at[:, pl.ds(2 * local, 2), :, lane_part(column)], own_sem.at[0]
    )
    own_force.start()
    send_table(1)
    send_table(2)

    relay_table(0)
    relay_again(0)
    finish_table(0)
    build(0, trans_1)
    product(trans_1, trans_1, trans_2)
    product(trans_2, trans_2, trans_4)
    product(trans_4, trans_4, trans_8)
    over_others(lambda offset: force_copy(offset).wait_recv())
    own_force.wait()

    def flat(x):
        return x.reshape(-1, state_width)

    def pairs(x):
        both = x.reshape(span, 2, SUBLANES, state_width)
        return both[:, 0], both[:, 1]

    def stacked(first, second):
        return jnp.stack([first, second], 1).reshape(rows, state_width)

    def relays():
        relay_table(1)
        relay_table(2)
        relay_again(1)
        relay_again(2)

    def smooth_tables():
        finish_table(1)
        build(1, smooth_1)
        product(smooth_1, smooth_1, smooth_2)
        product(smooth_2, smooth_2, smooth_4)
        product(smooth_4, smooth_4, smooth_8)
        finish_table(2)
        build(2, dyn_1)
        product(dyn_1, smooth_1, mix_1)

    @pl.when(late)
    def _():
        relays()

    current = flat(forcing[0])
    for step in range(1, short):
        current = times(current, trans_1) + flat(forcing[step])
    ends[...] = current.reshape(ends.shape)
    even, odd = pairs(current)
    sums[...] = times(flat(even), trans_4).reshape(sums.shape) + odd

    @pl.when(early)
    def _():
        firsts[0] = jnp.zeros_like(firsts[0])
        state = sums[0]
        for index in range(1, span):
            firsts[index] = state
            state = times(state, trans_8) + sums[index]
        edge[0] = state
        carry_copy(0).start()
        relays()

    @pl.when(late)
    def _():
        smooth_tables()
        carry_copy(0).wait_recv()
        state = carry[0]
        firsts[0] = state
        for index in range(1, span):
            state = times(state, trans_8) + sums[index - 1]
            firsts[index] = state

    even, _ = pairs(ends[...])
    first = firsts[...]
    second = times(flat(first), trans_4).reshape(sums.shape) + even
    current = stacked(first, second)
    for step in range(short):
        current = times(current, trans_1) + flat(forcing[step])
        states[step] = current.reshape(ends.shape)

    over_others(lambda offset: filtered_copy(offset).start())
    own_result(states, inbox_f, 1).start()

    @pl.when(early)
    def _():
        smooth_tables()

    for step in range(short):
        value = flat(states[step])
        mixed = times(value, mix_1)
        if step == short - 1:
            place = lax.broadcasted_iota(jnp.int32, mixed.shape, 0)
            at_end = jnp.logical_and(place >= rows - SUBLANES, late)
            mixed = jnp.where(at_end, jnp.zeros_like(mixed), mixed)
        drive[step] = (value - mixed).reshape(ends.shape)

    current = flat(drive[short - 1])
    for step in range(short - 2, -1, -1):
        current = times(current, smooth_1) + flat(drive[step])
    ends[...] = current.reshape(ends.shape)
    even, odd = pairs(current)
    sums[...] = times(flat(odd), smooth_4).reshape(sums.shape) + even

    @pl.when(late)
    def _():
        firsts[span - 1] = jnp.zeros_like(firsts[0])
        state = sums[span - 1]
        for index in range(span - 2, -1, -1):
            firsts[index] = state
            state = times(state, smooth_8) + sums[index]
        edge[1] = state
        carry_copy(1).start()

    @pl.when(early)
    def _():
        carry_copy(1).wait_recv()
        state = carry[1]
        firsts[span - 1] = state
        for index in range(span - 2, -1, -1):
            state = times(state, smooth_8) + sums[index + 1]
            firsts[index] = state

    _, odd = pairs(ends[...])
    last = firsts[...]
    before = times(flat(last), smooth_4).reshape(sums.shape) + odd
    current = stacked(before, last)
    for step in range(short - 1, -1, -1):
        current = times(current, smooth_1) + flat(drive[step])
        results[step] = current.reshape(ends.shape)

    over_others(lambda offset: smoothed_copy(offset).start())
    own_result(results, inbox_s, 2).start()

    def deliver(inbox, output):
        def one(step, _):
            for part in range(2):
                block = inbox[:, pl.ds(step, 1), part].reshape(members, tile_width)
                output[part * short + step] = block.T
            return 0

        lax.fori_loop(0, short, one, 0)

    over_others(lambda offset: filtered_copy(offset).wait_recv())
    own_result(states, inbox_f, 1).wait()
    deliver(inbox_f, filtered)
    over_others(lambda offset: smoothed_copy(offset).wait_recv())
    own_result(results, inbox_s, 2).wait()
    deliver(inbox_s, smoothed)

    for which in range(3):
        for what in range(5 if which in SPLIT else 3):
            table_copy(which, what).wait_send()
    over_others(lambda offset: force_copy(offset).wait_send())
    over_others(lambda offset: filtered_copy(offset).wait_send())
    over_others(lambda offset: smoothed_copy(offset).wait_send())

    @pl.when(early)
    def _():
        carry_copy(0).wait_send()

    @pl.when(late)
    def _():
        carry_copy(1).wait_send()


def member_body(ranks, columns, observed, gain, trans, dynamics, smooth_gain):
    steps, tile_width, members = observed.shape
    short = steps // 2
    span = ranks // 2
    group = span * columns
    width = columns * tile_width
    boxes = pltpu.VMEM((group, short, 2, SUBLANES, tile_width), jnp.float32)
    series = pltpu.VMEM((short, 2 * span, SUBLANES, width), jnp.float32)
    block = pltpu.VMEM((2 * span, SUBLANES, width), jnp.float32)
    small = pltpu.VMEM((span, SUBLANES, width), jnp.float32)
    edges = pltpu.VMEM((2, SUBLANES, width), jnp.float32)
    table = pltpu.VMEM((2, width, width), jnp.bfloat16)
    each = pltpu.SemaphoreType.DMA((group,))
    vmem = pl.BlockSpec(memory_space=pltpu.VMEM)
    return pl.pallas_call(
        partial(kernel, ranks, columns),
        out_shape=[jax.ShapeDtypeStruct(observed.shape, jnp.float32)] * 2,
        in_specs=[vmem] * 5,
        out_specs=[vmem] * 2,
        scratch_shapes=[
            boxes, series, series, series, series, boxes, boxes, block, small, small, edges, edges,
            pltpu.VMEM((3, columns, 3 * tile_width, tile_width), jnp.float32),
            table, table, table, table, table, table, table, table, table, table,
            pltpu.SemaphoreType.DMA((3, 5)),
            pltpu.SemaphoreType.DMA((3, 5)),
            pltpu.SemaphoreType.DMA((3,)),
            each, each, each, each, each, each,
            pltpu.SemaphoreType.DMA((2,)),
            pltpu.SemaphoreType.DMA((2,)),
            pltpu.SemaphoreType.DMA((3,)),
        ],
        compiler_params=pltpu.CompilerParams(
            collective_id=0, has_side_effects=True, vmem_limit_bytes=56 * 2**20
        ),
    )(observed, gain, trans, dynamics, smooth_gain)


def by_members(mesh, observed, gain, trans, dynamics, smooth_gain):
    ranks, columns = mesh.shape["tm"], mesh.shape["space"]
    steps, tile_width, members = observed.shape
    fits = (
        ranks % 2 == 0
        and ranks >= 4
        and members == ranks // 2 * columns * SUBLANES
        and steps % 2 == 0
        and steps >= 4
        and columns == 4
        and tile_width == 128
        and members == 128
    )
    if fits:
        return tuple(member_body(ranks, columns, observed, gain, trans, dynamics, smooth_gain))
    return body(observed, gain, trans, dynamics, smooth_gain)


def solution(mesh):
    return jax.shard_map(
        partial(by_members, mesh),
        mesh=mesh,
        in_specs=(
            P("tm", "space", None),
            P("space", None, None),
            P("space", None, None),
            P("space", None, None),
            P("space", None, None),
        ),
        out_specs=(P("tm", "space", None), P("tm", "space", None)),
        check_vma=False,
    )
```

time: 59.6 us -> 57.5 us (0.965)
  the two profiles are of different devices: /device:TPU:15 before, /device:TPU:7 now
where the time goes in v1:
time: 57.5 us; the launch traced here: 57.3 us
  Pallas kernels  53.9 us (94%)
  local copies, waits for them, and re-layouts  2.73 us (5%)
  between operations  0.65 us (1%)
    pallas_call x1, Pallas kernels, member_body(): pl.pallas_call(partial(kernel, ranks, columns), out_shape=[jax.ShapeDtype...  53.9 us
    unnamed x4, local copies, waits for them, and re-layouts  2.73 us

profile of v1, /device:TPU:7, one launch (start us, length us, event | category | flops | bytes accessed | tf_op | source)
XLA Modules:
  0.0 57.3 jit_solution(8706211385325888777)
XLA Ops:
  0.6 53.9 %shard_map.68 = (f32[8,128,128]{2,1,0:T(8,128)}, f32[8,128,128]{2,1,0:T(8,128)}) custom-call(f32[8,128,128]{2,1,0:T(8,128)} %observed.1, f32[1,128,128]{2,1,0:T(8,128)} %gain.1, f32[1,384,128]{2,1,0:T(8,128)} %trans.1, f32[1,384,128]{2,1,0:T(8,128)} %dynamics.1, f32[1,384,128]{2,1,0:T(8,128)} %smooth_gain.1), custom_call_target="tpu_custom_call" | custom-call | tf_op jit(solution)/shard_map/pallas_call | solution.py:534
  54.6 0.0 copy-start
  54.6 1.9 %copy.9 = f32[8,128,128]{2,1,0:T(8,128)} copy(f32[8,128,128]{2,1,0:T(8,128)} %get-tuple-element.4) | data formatting | bytes 1048576
  56.5 0.0 copy-done
  56.5 0.8 %copy.10 = f32[8,128,128]{2,1,0:T(8,128)} copy(f32[8,128,128]{2,1,0:T(8,128)S(1)} %copy-done) | data formatting | bytes 1048576
Async XLA Ops:
  54.6 1.9 %copy-start = (f32[8,128,128]{2,1,0:T(8,128)S(1)}, f32[8,128,128]{2,1,0:T(8,128)}, u32[]{:S(2)}) copy-start(f32[8,128,128]{2,1,0:T(8,128)} %get-tuple-element.5) | copy-start | bytes 1572868
